TPU v7x, 1024 devices: a whole 8x8x8 slice. The times are simulated.
1024 devices in a mesh: dp: 64 (over x_lo, z, core), tensor: 16 (over y, x_hi).
Axes of the slice: x: 8 (x_hi: 2, x_lo: 4; x = x_hi * 4 + x_lo), y: 8, z: 8, core: 2. Of those that a mesh axis runs over, the one named last changes fastest.
Arguments:
- queries: bfloat16 [28672, 8192], P('dp', 'tensor'), may hold values from -6 to 6
- features: bfloat16 [128, 384, 8192], P('dp', None, 'tensor'), may hold values from -6 to 6
- kv_weight: bfloat16 [8192, 2048], P('tensor'), may hold values from -0.0625 to 0.0625
- q_gain: float32 [128], replicated, may hold values from 0.5 to 2
- k_gain: float32 [128], replicated, may hold values from 0.5 to 2
- counts: int32 [128], replicated, may hold values from 1 to 16, as said below
- owner: int32 [128], replicated, may hold values from 0 to 127, as said below
Outputs:
- attended: bfloat16 [28672, 8192], P('dp', 'tensor')
Inputs may be any that keep to these rules, and one draw needn't show every extreme that they name: `counts`: every sample has 1 to 16 images; in every draw some sample has 16 and some has one. `owner`: there are 2 different shifts c_j, each from 0 to the number of dp indices minus 1; sample s = e * 2 + j goes to slot ((e + c_j) modulo the number of dp indices) * 2 + j, with the same c_j for every e.
All inputs are finite; a program needn't handle non-finite values.
Results may differ from a plain program's by a relative error of at most 0.028.
Values may be sent and summed in bfloat16 or wider, within the bound.
A program may use at most 64 MiB of HBM per device.

v0:
```python
import math

import jax
import jax.numpy as jnp
from jax import lax
from jax.sharding import Mesh
from jax.sharding import PartitionSpec as P

KVH = 8
HD = 128
PATCH = 24
TENSOR = ("tensor_0", "tensor_1")


def own_rows(terms, axes):
    so_far = terms.astype(jnp.bfloat16)
    for axis in axes:
        so_far = lax.psum_scatter(so_far, axis, scatter_dimension=0, tiled=True)
    return so_far.astype(jnp.float32)


def shifted(value, axis, by):
    length = lax.axis_size(axis)
    return lax.ppermute(value, axis, [(i, (i + by) % length) for i in range(length)])


def normalize_axis(values_in, gain, axis):
    scale = lax.rsqrt(jnp.mean(values_in * values_in, axis=axis, keepdims=True) + 1e-05)
    return values_in * scale * gain


def shards(queries, features, kv_weight, q_gain, k_gain, counts, owner):
    samples_here = features.shape[0]
    token_count = features.shape[1]
    shard_count = lax.axis_size("dp")
    tensor_count = lax.axis_size(TENSOR)
    my_index = lax.axis_index("dp")
    local_width = kv_weight.shape[1] // tensor_count
    repeats = max(1, 2 * HD // local_width)
    head_rows = local_width * repeats
    weight_used = jnp.repeat(kv_weight.reshape(kv_weight.shape[0], KVH, 2 * HD), repeats, axis=1)
    weight_used = weight_used.reshape(kv_weight.shape[0], KVH * repeats * 2 * HD)
    shifts = owner[:samples_here] // samples_here
    source = (my_index - shifts) % shard_count * samples_here + jnp.arange(
        samples_here, dtype=jnp.int32
    )
    matches = jnp.arange(counts.shape[0], dtype=jnp.int32)[None, :] == source[:, None]
    slot_count = jnp.sum(jnp.where(matches, counts[None, :], 0), axis=1)
    levels = 0
    while 1 << levels < shard_count:
        levels += 1
    kv_heads = head_rows // (2 * HD)
    flat = features.reshape(-1, features.shape[2])
    summed = own_rows(
        lax.dot_general(
            weight_used, flat, (((0,), (1,)), ((), ())), preferred_element_type=jnp.float32
        ),
        TENSOR,
    )
    split = summed.reshape(head_rows, samples_here, token_count).reshape(
        kv_heads, 2, HD, samples_here, token_count
    )
    normed = normalize_axis(split[:, 0], k_gain[None, :, None, None], 1)
    joined = jnp.stack([normed, split[:, 1]], axis=1)
    ready = joined.reshape(head_rows, samples_here, token_count).astype(jnp.bfloat16)
    for level in range(levels):
        moved = shifted(ready, "dp", 1 << level)
        take = shifts // (1 << level) % 2 == 1
        ready = jnp.where(take[None, :, None], moved, ready)
    split = ready.reshape(kv_heads, 2, HD, samples_here, token_count)
    key_heads = split[:, 0]
    value_heads = split[:, 1]
    query_rows = queries.shape[0]
    head_count = queries.shape[1] // HD
    text_len = query_rows // samples_here
    query_float = queries.astype(jnp.float32).reshape(
        samples_here, text_len, kv_heads, head_count // kv_heads, HD
    )
    query_normed = (normalize_axis(query_float, q_gain, -1) / math.sqrt(HD)).astype(jnp.bfloat16)
    scores = jnp.einsum(
        "stgad,gdsr->sgatr", query_normed, key_heads, preferred_element_type=jnp.float32
    )
    valid_keys = jnp.arange(token_count, dtype=jnp.int32)[None, :] < (slot_count * PATCH)[:, None]
    exponent = jnp.where(valid_keys[:, None, None, None, :], jnp.exp(scores), 0.0)
    weights = (exponent / jnp.sum(exponent, axis=-1, keepdims=True)).astype(jnp.bfloat16)
    context = jnp.einsum(
        "sgatr,gdsr->stgad", weights, value_heads, preferred_element_type=jnp.float32
    )
    return context.astype(jnp.bfloat16).reshape(query_rows, head_count * HD)


def solution(mesh):
    torus = Mesh(mesh.devices.reshape(mesh.shape["dp"], 8, 2), ("dp", "tensor_0", "tensor_1"))
    in_specs = (P("dp", TENSOR), P("dp", None, TENSOR), P(TENSOR, None), P(), P(), P(), P())
    out_specs = P("dp", TENSOR)
    return jax.shard_map(
        shards, mesh=torus, in_specs=in_specs, out_specs=out_specs, check_vma=False
    )
```

profile of v0, /device:TPU:384, one launch (start us, length us, event | category | flops | bytes accessed | tf_op | source)
XLA Modules:
  0.0 280.1 jit_solution(2659831199451697963)
XLA Ops:
  6.5 2.3 copy.36
  8.9 3.7 %broadcast_in_dim.83 = bf16[512,8,2,256]{3,2,1,0:T(2,128)(2,1)} broadcast(bf16[512,8,256]{2,1,0:T(8,128)(2,1)S(1)} %bitcast.70), dimensions={0,1,3} | broadcast | bytes 6291456 | tf_op jit(solution)/shard_map/broadcast_in_dim | solution.py:41
  12.6 7.8 %reshape_reshape.7 = bf16[512,4096]{1,0:T(8,128)(2,1)} reshape(bf16[512,8,2,256]{3,2,1,0:T(2,128)(2,1)} %broadcast_in_dim.83) | data formatting | bytes 8388608 | tf_op jit(solution)/shard_map/reshape;reshape | solution.py:42
  20.3 8.3 %convolution_convert_fusion = bf16[4096,768]{1,0:T(8,128)(2,1)} fusion(bf16[512,4096]{1,0:T(8,128)(2,1)} %reshape_reshape.7, bf16[768,512]{1,0:T(8,128)(2,1)S(1)} %bitcast.69), kind=kOutput, calls=%fused_computation | convolution fusion | flops 3224371200 | bytes 11272192 | tf_op jit(solution)/shard_map/dot_general | solution.py:55
  28.8 87.3 %reduce-scatter.3.cloned.1.call-done = bf16[512,768]{1,0:T(8,128)(2,1)} async-done(((bf16[4096,768]{1,0:T(8,128)(2,1)}), bf16[512,768]{1,0:T(8,128)(2,1)}) %reduce-scatter.3.cloned.1.call-update) | async-done | bytes 786448 | tf_op jit(solution)/shard_map/reduce_scatter | solution.py:18
  116.1 39.0 %reduce-scatter.5.cloned.1.call-done = bf16[256,768]{1,0:T(8,128)(2,1)} async-done(((bf16[512,768]{1,0:T(8,128)(2,1)}), bf16[256,768]{1,0:T(8,128)(2,1)}) %reduce-scatter.5.cloned.1.call-update) | async-done | bytes 393232 | tf_op jit(solution)/shard_map/reduce_scatter | solution.py:18
  155.0 1.1 reshape_reshape.8
  157.4 2.1 collective-permute-start
  159.6 7.1 %collective-permute-done = bf16[256,2,384]{2,0,1:T(8,128)(2,1)S(1)} collective-permute-done((bf16[256,2,384]{2,0,1:T(8,128)(2,1)S(1)}, bf16[256,2,384]{2,0,1:T(8,128)(2,1)S(1)}, u32[]{:S(2)}, u32[]{:S(2)}) %collective-permute-start) | collective-permute-done | bytes 393248 | tf_op jit(solution)/shard_map/ppermute | solution.py:24
  166.8 6.2 %collective-permute-start.1 = (bf16[256,2,384]{2,0,1:T(8,128)(2,1)S(1)}, bf16[256,2,384]{2,0,1:T(8,128)(2,1)S(1)}, u32[]{:S(2)}, u32[]{:S(2)}) collective-permute-start(bf16[256,2,384]{2,0,1:T(8,128)(2,1)S(1)} %broadcast_select_fusion), channel_id=1, source_target_pairs={{0,32},{16,48},{32,64},{48,80},{64,96},{80,112},{96,128},{112,144}... | collective-permute-start | bytes 1179656 | tf_op jit(solution)/shard_map/ppermute | solution.py:24
  173.0 7.4 %collective-permute-done.1 = bf16[256,2,384]{2,0,1:T(8,128)(2,1)S(1)} collective-permute-done((bf16[256,2,384]{2,0,1:T(8,128)(2,1)S(1)}, bf16[256,2,384]{2,0,1:T(8,128)(2,1)S(1)}, u32[]{:S(2)}, u32[]{:S(2)}) %collective-permute-start.1) | collective-permute-done | bytes 393248 | tf_op jit(solution)/shard_map/ppermute | solution.py:24
  180.5 3.2 %collective-permute-start.2 = (bf16[256,2,384]{2,0,1:T(8,128)(2,1)S(1)}, bf16[256,2,384]{2,0,1:T(8,128)(2,1)S(1)}, u32[]{:S(2)}, u32[]{:S(2)}) collective-permute-start(bf16[256,2,384]{2,0,1:T(8,128)(2,1)S(1)} %broadcast_select_fusion.1), channel_id=1, source_target_pairs={{0,64},{16,80},{32,96},{48,112},{64,128},{80,144},{96,160},{112,17... | collective-permute-start | bytes 1179656 | tf_op jit(solution)/shard_map/ppermute | solution.py:24
  183.7 18.7 %collective-permute-done.2 = bf16[256,2,384]{2,0,1:T(8,128)(2,1)S(1)} collective-permute-done((bf16[256,2,384]{2,0,1:T(8,128)(2,1)S(1)}, bf16[256,2,384]{2,0,1:T(8,128)(2,1)S(1)}, u32[]{:S(2)}, u32[]{:S(2)}) %collective-permute-start.2) | collective-permute-done | bytes 393248 | tf_op jit(solution)/shard_map/ppermute | solution.py:24
  202.5 25.5 %collective-permute-start.3 = (bf16[256,2,384]{2,0,1:T(8,128)(2,1)S(1)}, bf16[256,2,384]{2,0,1:T(8,128)(2,1)S(1)}, u32[]{:S(2)}, u32[]{:S(2)}) collective-permute-start(bf16[256,2,384]{2,0,1:T(8,128)(2,1)S(1)} %broadcast_select_fusion.2), channel_id=1, source_target_pairs={{0,128},{16,144},{32,160},{48,176},{64,192},{80,208},{96,224},{112... | collective-permute-start | bytes 1179656 | tf_op jit(solution)/shard_map/ppermute | solution.py:24
  228.0 5.3 %collective-permute-done.3 = bf16[256,2,384]{2,0,1:T(8,128)(2,1)S(1)} collective-permute-done((bf16[256,2,384]{2,0,1:T(8,128)(2,1)S(1)}, bf16[256,2,384]{2,0,1:T(8,128)(2,1)S(1)}, u32[]{:S(2)}, u32[]{:S(2)}) %collective-permute-start.3) | collective-permute-done | bytes 393248 | tf_op jit(solution)/shard_map/ppermute | solution.py:24
  233.3 0.9 broadcast_select_fusion.3
  234.2 7.4 %collective-permute-start.4 = (bf16[256,2,384]{2,0,1:T(8,128)(2,1)}, bf16[256,2,384]{2,0,1:T(8,128)(2,1)}, u32[]{:S(2)}, u32[]{:S(2)}) collective-permute-start(bf16[256,2,384]{2,0,1:T(8,128)(2,1)} %broadcast_select_fusion.3), channel_id=1, source_target_pairs={{0,256},{16,272},{32,288},{48,304},{64,320},{80,336},{96,352},{112... | collective-permute-start | bytes 1179656 | tf_op jit(solution)/shard_map/ppermute | solution.py:24
  243.0 0.8 fusion.22
  243.8 7.2 %collective-permute-done.4 = bf16[256,2,384]{2,0,1:T(8,128)(2,1)} collective-permute-done((bf16[256,2,384]{2,0,1:T(8,128)(2,1)}, bf16[256,2,384]{2,0,1:T(8,128)(2,1)}, u32[]{:S(2)}, u32[]{:S(2)}) %collective-permute-start.4) | collective-permute-done | bytes 393248 | tf_op jit(solution)/shard_map/ppermute | solution.py:24
  251.0 1.2 broadcast_select_fusion.4
  252.2 8.0 %collective-permute-start.5 = (bf16[256,2,384]{2,0,1:T(8,128)(2,1)S(1)}, bf16[256,2,384]{2,0,1:T(8,128)(2,1)S(1)}, u32[]{:S(2)}, u32[]{:S(2)}) collective-permute-start(bf16[256,2,384]{2,0,1:T(8,128)(2,1)S(1)} %broadcast_select_fusion.4), channel_id=1, source_target_pairs={{0,512},{16,528},{32,544},{48,560},{64,576},{80,592},{96,608},{112... | collective-permute-start | bytes 1179656 | tf_op jit(solution)/shard_map/ppermute | solution.py:24
  260.3 9.9 %collective-permute-done.5 = bf16[256,2,384]{2,0,1:T(8,128)(2,1)S(1)} collective-permute-done((bf16[256,2,384]{2,0,1:T(8,128)(2,1)S(1)}, bf16[256,2,384]{2,0,1:T(8,128)(2,1)S(1)}, u32[]{:S(2)}, u32[]{:S(2)}) %collective-permute-start.5) | collective-permute-done | bytes 393248 | tf_op jit(solution)/shard_map/ppermute | solution.py:24
  270.3 1.1 bitcast_reduce_fusion
  272.4 0.8 copy.49
  (36 shorter events, 4.3 us)
Async XLA Ops:
  6.5 13.8 %copy-start = (bf16[2,384,512]{2,1,0:T(8,128)(2,1)S(1)}, bf16[2,384,512]{2,1,0:T(8,128)(2,1)}, u32[]{:S(2)}) copy-start(bf16[2,384,512]{2,1,0:T(8,128)(2,1)} %param.8) | copy-start | bytes 2359300
  6.5 109.5 %reduce-scatter.3.cloned.1.call-start = ((), (), s32[]{:S(2)}) async-start(), calls=%async_computation.2 | async-start | bytes 7077888 | tf_op jit(solution)/shard_map/reduce_scatter | solution.py:18
  28.7 127.9 %copy-start.2 = (f32[128]{0:T(128)S(1)}, f32[128]{0:T(128)}, u32[]{:S(2)}) copy-start(f32[128]{0:T(128)} %param.11) | copy-start | bytes 1540
  28.7 130.8 %copy-start.4 = (s32[128]{0:T(128)S(1)}, s32[128]{0:T(128)}, u32[]{:S(2)}) copy-start(s32[128]{0:T(128)} %param.13) | copy-start | bytes 1540
  28.7 126.3 %reduce-scatter.5.cloned.1.call-start = ((), (), s32[]{:S(2)}) async-start(), calls=%async_computation.3 | async-start | bytes 1179648 | tf_op jit(solution)/shard_map/reduce_scatter | solution.py:18
  157.4 84.2 %copy-start.1 = (bf16[448,512]{1,0:T(8,128)(2,1)S(1)}, bf16[448,512]{1,0:T(8,128)(2,1)}, u32[]{:S(2)}) copy-start(bf16[448,512]{1,0:T(8,128)(2,1)} %param.7) | copy-start | bytes 1376260
  157.4 9.2 %collective-permute-start = (bf16[256,2,384]{2,0,1:T(8,128)(2,1)S(1)}, bf16[256,2,384]{2,0,1:T(8,128)(2,1)S(1)}, u32[]{:S(2)}, u32[]{:S(2)}) collective-permute-start(bf16[256,2,384]{2,0,1:T(8,128)(2,1)S(1)} %bitcast.73), channel_id=1, source_target_pairs={{0,16},{16,32},{32,48},{48,64},{64,80},{80,96},{96,112},{112,128},... | collective-permute-start | bytes 1179656 | tf_op jit(solution)/shard_map/ppermute | solution.py:24
  166.8 13.6 %collective-permute-start.1 = (bf16[256,2,384]{2,0,1:T(8,128)(2,1)S(1)}, bf16[256,2,384]{2,0,1:T(8,128)(2,1)S(1)}, u32[]{:S(2)}, u32[]{:S(2)}) collective-permute-start(bf16[256,2,384]{2,0,1:T(8,128)(2,1)S(1)} %broadcast_select_fusion), channel_id=1, source_target_pairs={{0,32},{16,48},{32,64},{48,80},{64,96},{80,112},{96,128},{112,144}... | collective-permute-start | bytes 1179656 | tf_op jit(solution)/shard_map/ppermute | solution.py:24
  180.5 21.9 %collective-permute-start.2 = (bf16[256,2,384]{2,0,1:T(8,128)(2,1)S(1)}, bf16[256,2,384]{2,0,1:T(8,128)(2,1)S(1)}, u32[]{:S(2)}, u32[]{:S(2)}) collective-permute-start(bf16[256,2,384]{2,0,1:T(8,128)(2,1)S(1)} %broadcast_select_fusion.1), channel_id=1, source_target_pairs={{0,64},{16,80},{32,96},{48,112},{64,128},{80,144},{96,160},{112,17... | collective-permute-start | bytes 1179656 | tf_op jit(solution)/shard_map/ppermute | solution.py:24
  202.5 30.8 %collective-permute-start.3 = (bf16[256,2,384]{2,0,1:T(8,128)(2,1)S(1)}, bf16[256,2,384]{2,0,1:T(8,128)(2,1)S(1)}, u32[]{:S(2)}, u32[]{:S(2)}) collective-permute-start(bf16[256,2,384]{2,0,1:T(8,128)(2,1)S(1)} %broadcast_select_fusion.2), channel_id=1, source_target_pairs={{0,128},{16,144},{32,160},{48,176},{64,192},{80,208},{96,224},{112... | collective-permute-start | bytes 1179656 | tf_op jit(solution)/shard_map/ppermute | solution.py:24
  234.2 16.8 %collective-permute-start.4 = (bf16[256,2,384]{2,0,1:T(8,128)(2,1)}, bf16[256,2,384]{2,0,1:T(8,128)(2,1)}, u32[]{:S(2)}, u32[]{:S(2)}) collective-permute-start(bf16[256,2,384]{2,0,1:T(8,128)(2,1)} %broadcast_select_fusion.3), channel_id=1, source_target_pairs={{0,256},{16,272},{32,288},{48,304},{64,320},{80,336},{96,352},{112... | collective-permute-start | bytes 1179656 | tf_op jit(solution)/shard_map/ppermute | solution.py:24
  242.0 28.3 %copy-start.3 = (f32[128]{0:T(128)S(1)}, f32[128]{0:T(128)}, u32[]{:S(2)}) copy-start(f32[128]{0:T(128)} %param.10) | copy-start | bytes 1540
  252.2 17.9 %collective-permute-start.5 = (bf16[256,2,384]{2,0,1:T(8,128)(2,1)S(1)}, bf16[256,2,384]{2,0,1:T(8,128)(2,1)S(1)}, u32[]{:S(2)}, u32[]{:S(2)}) collective-permute-start(bf16[256,2,384]{2,0,1:T(8,128)(2,1)S(1)} %broadcast_select_fusion.4), channel_id=1, source_target_pairs={{0,512},{16,528},{32,544},{48,560},{64,576},{80,592},{96,608},{112... | collective-permute-start | bytes 1179656 | tf_op jit(solution)/shard_map/ppermute | solution.py:24
Sparse Core Ops, SparseCore 0:
  28.8 87.1 reduce-scatter.2
  119.4 35.5 reduce-scatter.4
where the time goes:
time: 281 us; the launch traced here: 280 us
  waiting for transfers between devices  182 us (65%)
  starting transfers between devices  52.3 us (19%)
  local copies, waits for them, and re-layouts  16.9 us (6%)
  between operations  13.6 us (5%)
  matrix products  10.2 us (4%)
  other arithmetic  5.24 us (2%)
    reduce_scatter x2, waiting for transfers between devices, own_rows(): so_far = lax.psum_scatter(so_far, axis, scatter_dimension=0, tiled=True)  126 us
    ppermute x6, waiting for transfers between devices, shifted(): lax.ppermute(value, axis, [(i, (i + by) % length) for i in range(length)])  55.6 us
    ppermute x6, starting transfers between devices, shifted(): lax.ppermute(value, axis, [(i, (i + by) % length) for i in range(length)])  52.2 us
    dot_general x1, matrix products, shards(): lax.dot_general(weight_used, flat, (((0,), (1,)), ((), ())), preferred_el...  8.35 us
    another operation x1, local copies, waits for them, and re-layouts, shards(): weight_used.reshape(kv_weight.shape[0], KVH * repeats * 2 * HD)  7.77 us
  transfers between devices with their start and end apart: 8, of which 8 were waited for; matrix products, arithmetic and copies ran while one was open for 1% of the time, Pallas kernels for 0%

commit v1 on v0

v1 whole, which is shorter than its diff:
```python
import functools
import math

import jax
import jax.numpy as jnp
from jax import lax
from jax.experimental import pallas as pl
from jax.experimental.pallas import tpu as pltpu
from jax.sharding import Mesh
from jax.sharding import PartitionSpec as P

KVH = 8
HD = 128
PATCH = 24
PIECES = 8
COPIES = 18
DP = ("x_lo", "z", "core")
TENSOR = ("y", "x_hi")
MESH = pl.DeviceIdType.MESH


def wrap(value, size):
    return lax.rem(value + 2 * size, size)


def exchange(
    pieces, owner_ref, feat_ref, weight_ref, gain_ref, out_ref,
    partner, chosen, first, left0, right0, left1, right1, left, right,
    summed, cross, ready, near, turned, far, spun, side, twin_k, twin_v,
    send_sem, recv_sem, core_send, core_recv,
):
    x_lo, z, core = lax.axis_index("x_lo"), lax.axis_index("z"), lax.axis_index("core")
    y, x_hi = lax.axis_index("y"), lax.axis_index("x_hi")
    x = x_hi * 4 + x_lo
    samples = feat_ref.shape[0]
    tokens = feat_ref.shape[1]
    rows = samples * tokens // pieces
    per_sample = pieces // samples

    def at_x(by):
        there = wrap(x + by, 8)
        return {"x_lo": lax.rem(there, 4), "x_hi": there // 4}

    def at_y(by):
        return {"y": wrap(y + by, 8)}

    def at_z(by):
        return {"z": wrap(z + by, 8)}

    other_core = {"core": 1 - core}

    barrier = pltpu.get_barrier_semaphore()
    peers = [at_y(-1), at_y(1), at_x(-2), at_x(2), at_x(-1), at_x(1)]
    peers += [at_z(-1), at_z(1), at_z(-3), at_z(3), other_core]
    for peer in peers:
        pl.semaphore_signal(barrier, inc=1, device_id=peer, device_id_type=MESH)
    pl.semaphore_wait(barrier, len(peers))

    core_copies = []
    for j in range(samples):
        copy = pltpu.make_async_remote_copy(
            src_ref=feat_ref.at[j], dst_ref=partner.at[j],
            send_sem=core_send.at[j], recv_sem=core_recv.at[j],
            device_id=other_core, device_id_type=MESH,
        )
        copy.start()
        core_copies.append(copy)

    place = z * 2 + core
    plan = []
    for j in range(samples):
        shift = owner_ref[j] // samples
        swap = lax.rem(shift, 2)
        low = lax.rem(shift, 16)
        borrow = jnp.where(place < low, 1, 0)
        along_z = lax.rem(lax.rem(shift // 2, 8) + swap * (1 - core), 8)
        along_x = lax.rem(shift // 16 + borrow + 2, 4)
        plan.append((swap, along_z, along_x))

    copies = {}

    def send(piece, number, source, target, device):
        copy = pltpu.make_async_remote_copy(
            src_ref=source, dst_ref=target,
            send_sem=send_sem.at[piece * COPIES + number],
            recv_sem=recv_sem.at[piece * COPIES + number],
            device_id=device, device_id_type=MESH,
        )
        copy.start()
        copies[piece, number] = copy

    def arrive(piece, *numbers):
        for number in numbers:
            copies[piece, number].wait_recv()

    def partial(piece, by):
        head = wrap(y + by, 8)
        columns = pl.ds(pl.multiple_of(head * 2 * HD, 2 * HD), 2 * HD)
        return jnp.dot(
            chosen[pl.ds(piece * rows, rows), :], weight_ref[:, columns],
            preferred_element_type=jnp.float32,
        )

    def widen(value):
        return value.astype(jnp.float32)

    def narrow(value):
        return value.astype(jnp.bfloat16)

    def start_piece(p):
        j = p // per_sample
        if p % per_sample == 0:
            core_copies[j].wait_recv()
            swapped = jnp.full((tokens, 1), plan[j][0], jnp.int32) == 1
            chosen[pl.ds(j * tokens, tokens), :] = jnp.where(swapped, partner[j], feat_ref[j])
        first[p] = narrow(partial(p, 4))
        send(p, 0, first.at[p, :, pl.ds(0, HD)], left0.at[p], at_y(-1))
        send(p, 1, first.at[p, :, pl.ds(HD, HD)], right0.at[p], at_y(1))

    def second(p):
        to_left, to_right = partial(p, -3), partial(p, 3)
        arrive(p, 0, 1)
        left1[p, :, pl.ds(0, HD)] = narrow(to_left[:, :HD] + widen(left0[p]))
        left1[p, :, pl.ds(HD, HD)] = narrow(to_left[:, HD:])
        send(p, 2, left1.at[p], left.at[p, 0], at_y(-1))
        right1[p, :, pl.ds(0, HD)] = narrow(to_right[:, :HD])
        right1[p, :, pl.ds(HD, HD)] = narrow(to_right[:, HD:] + widen(right0[p]))
        send(p, 3, right1.at[p], right.at[p, 0], at_y(1))

    def later(p, step):
        to_left, to_right = partial(p, step - 3), partial(p, 3 - step)
        arrive(p, 2 * step, 2 * step + 1)
        left[p, step - 1] = narrow(to_left + widen(left[p, step - 1]))
        send(p, 2 * step + 2, left.at[p, step - 1], left.at[p, step], at_y(-1))
        right[p, step - 1] = narrow(to_right + widen(right[p, step - 1]))
        send(p, 2 * step + 3, right.at[p, step - 1], right.at[p, step], at_y(1))

    def own(p):
        mine = partial(p, 0)
        arrive(p, 6, 7)
        summed[p] = narrow(mine + widen(left[p, 2]) + widen(right[p, 2]))
        send(p, 8, summed.at[p], cross.at[p, 0], at_x(2))
        send(p, 9, summed.at[p], cross.at[p, 1], at_x(-2))

    def normed(p):
        arrive(p, 8, 9)
        total = widen(cross[p, 0]) + widen(cross[p, 1])
        keys = total[:, :HD]
        scale = lax.rsqrt(jnp.mean(keys * keys, axis=-1, keepdims=True) + 1e-05)
        ready[p, :, pl.ds(0, HD)] = narrow(keys * scale * gain_ref[...])
        ready[p, :, pl.ds(HD, HD)] = narrow(total[:, HD:])
        send(p, 10, ready.at[p], near.at[p, 0], at_z(1))
        send(p, 11, ready.at[p], near.at[p, 1], at_z(-1))

    def pick(index, options):
        mask = jnp.full((rows, 1), index, jnp.int32)
        result = options[0]
        for number in range(1, len(options)):
            result = jnp.where(mask == number, options[number], result)
        return result

    def turn_near(p):
        arrive(p, 10, 11)
        s = plan[p // per_sample][1]
        plus = (s == 1) | (s == 4) | (s == 6)
        minus = (s == 2) | (s == 7)
        index = jnp.where(plus, 1, jnp.where(minus, 2, 0))
        turned[p] = pick(index, [ready[p], near[p, 0], near[p, 1]])
        send(p, 12, turned.at[p], far.at[p, 0], at_z(3))
        send(p, 13, turned.at[p], far.at[p, 1], at_z(-3))

    def turn_far(p):
        arrive(p, 12, 13)
        s = plan[p // per_sample][1]
        plus = (s == 2) | (s == 3) | (s == 4)
        minus = (s == 5) | (s == 6)
        index = jnp.where(plus, 1, jnp.where(minus, 2, 0))
        spun[p] = pick(index, [turned[p], far[p, 0], far[p, 1]])
        send(p, 14, spun.at[p], side.at[p, 0], at_x(1))
        send(p, 15, spun.at[p], side.at[p, 1], at_x(-1))
        send(p, 16, spun.at[p, :, pl.ds(0, HD)], twin_k.at[p], at_x(2))
        send(p, 17, spun.at[p, :, pl.ds(HD, HD)], twin_v.at[p], at_x(-2))

    def finish(p):
        arrive(p, 14, 15, 16, 17)
        u = plan[p // per_sample][2]
        for half, twin in enumerate((twin_k, twin_v)):
            part = pl.ds(half * HD, HD)
            out_ref[pl.ds(p * rows, rows), part] = pick(
                u, [spun[p, :, part], side[p, 0, :, part], twin[p], side[p, 1, :, part]]
            )

    stages = [start_piece, second, lambda p: later(p, 1), lambda p: later(p, 2), own, normed]
    stages += [turn_near, turn_far, finish]
    for t in range(pieces + len(stages) - 1):
        for number in reversed(range(len(stages))):
            if 0 <= t - number < pieces:
                stages[number](t - number)
    for copy in core_copies:
        copy.wait_send()
    for copy in copies.values():
        copy.wait_send()


def keys_and_values(features, kv_weight, k_gain, owner):
    samples, tokens, width = features.shape
    total = samples * tokens
    rows = total // PIECES
    wide, half = (rows, 2 * HD), (rows, HD)

    def buffers(*shape):
        return pltpu.VMEM((PIECES, *shape), jnp.bfloat16)

    vmem = pl.BlockSpec(memory_space=pltpu.VMEM)
    return pl.pallas_call(
        functools.partial(exchange, PIECES),
        out_shape=jax.ShapeDtypeStruct((total, 2 * HD), jnp.bfloat16),
        in_specs=[pl.BlockSpec(memory_space=pltpu.SMEM), vmem, vmem, vmem],
        out_specs=vmem,
        scratch_shapes=[
            pltpu.VMEM((samples, tokens, width), jnp.bfloat16),
            pltpu.VMEM((total, width), jnp.bfloat16),
            buffers(*wide), buffers(*half), buffers(*half), buffers(*wide), buffers(*wide),
            buffers(3, *wide), buffers(3, *wide),
            buffers(*wide), buffers(2, *wide), buffers(*wide), buffers(2, *wide),
            buffers(*wide), buffers(2, *wide), buffers(*wide), buffers(2, *wide),
            buffers(*half), buffers(*half),
            pltpu.SemaphoreType.DMA((PIECES * COPIES,)),
            pltpu.SemaphoreType.DMA((PIECES * COPIES,)),
            pltpu.SemaphoreType.DMA((samples,)),
            pltpu.SemaphoreType.DMA((samples,)),
        ],
        compiler_params=pltpu.CompilerParams(
            collective_id=0, has_side_effects=True, vmem_limit_bytes=48 * 1024 * 1024
        ),
        name="exchange",
    )(owner, features, kv_weight, k_gain.reshape(1, HD))


def normalize(values_in, gain):
    scale = lax.rsqrt(jnp.mean(values_in * values_in, axis=-1, keepdims=True) + 1e-05)
    return values_in * scale * gain


def shards(queries, features, kv_weight, q_gain, k_gain, counts, owner):
    samples, tokens = features.shape[:2]
    both = keys_and_values(features, kv_weight, k_gain, owner)
    both = both.reshape(samples, tokens, 2 * HD)
    key_heads, value_heads = both[..., :HD], both[..., HD:]
    shifts = owner[:samples] // samples
    shard_count = lax.axis_size(DP)
    source = (lax.axis_index(DP) - shifts) % shard_count * samples
    source = source + jnp.arange(samples, dtype=jnp.int32)
    matches = jnp.arange(counts.shape[0], dtype=jnp.int32)[None, :] == source[:, None]
    slot_count = jnp.sum(jnp.where(matches, counts[None, :], 0), axis=1)
    query_rows = queries.shape[0]
    heads = queries.shape[1] // HD
    text_len = query_rows // samples
    query_float = queries.astype(jnp.float32).reshape(samples, text_len, heads, HD)
    query_normed = (normalize(query_float, q_gain) / math.sqrt(HD)).astype(jnp.bfloat16)
    scores = jnp.einsum(
        "stad,srd->satr", query_normed, key_heads, preferred_element_type=jnp.float32
    )
    valid_keys = jnp.arange(tokens, dtype=jnp.int32)[None, :] < (slot_count * PATCH)[:, None]
    exponent = jnp.where(valid_keys[:, None, None, :], jnp.exp(scores), 0.0)
    weights = (exponent / jnp.sum(exponent, axis=-1, keepdims=True)).astype(jnp.bfloat16)
    context = jnp.einsum(
        "satr,srd->stad", weights, value_heads, preferred_element_type=jnp.float32
    )
    return context.astype(jnp.bfloat16).reshape(query_rows, heads * HD)


def solution(mesh):
    torus = Mesh(mesh.devices.reshape(4, 8, 2, 8, 2), (*DP, *TENSOR))
    in_specs = (P(DP, TENSOR), P(DP, None, TENSOR), P(TENSOR, None), P(), P(), P(), P())
    return jax.shard_map(
        shards, mesh=torus, in_specs=in_specs, out_specs=P(DP, TENSOR), check_vma=False
    )
```

time: 281 us -> 112 us (0.40)
  the two profiles are of different devices: /device:TPU:384 before, /device:TPU:14 now
where the time goes in v1:
time: 112 us
  Pallas kernels  103 us (92%)
  local copies, waits for them, and re-layouts  5.4 us (5%)
  other arithmetic  2.73 us (2%)
  matrix products  1.38 us (1%)
    pallas_call x1, Pallas kernels, keys_and_values(): pl.pallas_call(functools.partial(exchange, PIECES), out_shape=jax.ShapeDt...  103 us
    unnamed x13, local copies, waits for them, and re-layouts  4.88 us

profile of v1, /device:TPU:14, one launch (start us, length us, event | category | flops | bytes accessed | tf_op | source)
XLA Modules:
  0.0 112.1 jit_solution(4029243256637845923)
XLA Ops:
  0.0 0.7 fusion.13
  0.7 0.8 fusion.11
  1.5 0.1 iota_compare_fusion
  1.6 0.0 copy-start
  1.6 1.6 %copy-done = bf16[512,2048]{1,0:T(8,128)(2,1)S(1)} copy-done((bf16[512,2048]{1,0:T(8,128)(2,1)S(1)}, bf16[512,2048]{1,0:T(8,128)(2,1)}, u32[]{:S(2)}) %copy-start) | copy-done | bytes 2097176
  3.2 0.0 copy-start.1
  3.2 1.1 %copy-done.1 = bf16[2,384,512]{2,1,0:T(8,128)(2,1)S(1)} copy-done((bf16[2,384,512]{2,1,0:T(8,128)(2,1)S(1)}, bf16[2,384,512]{2,1,0:T(8,128)(2,1)}, u32[]{:S(2)}) %copy-start.1) | copy-done | bytes 786456
  4.3 0.0 copy-start.2
  4.3 0.7 copy-done.2
  5.0 0.0 copy-start.3
  5.0 0.7 copy-done.3
  5.6 0.0 copy-start.4
  5.6 0.0 copy-start.5
  5.6 102.5 %exchange.1 = bf16[768,256]{1,0:T(8,128)(2,1)S(1)} custom-call(s32[128]{0:T(128)S(1)} %copy-done.2, bf16[2,384,512]{2,1,0:T(8,128)(2,1)S(1)} %copy-done.1, bf16[512,2048]{1,0:T(8,128)(2,1)S(1)} %copy-done, f32[1,128]{1,0:T(1,128)S(1)} %bitcast.33), custom_call_target="tpu_custom_call" | custom-call | tf_op jit(solution)/shard_map/exchange/pallas_call | solution.py:215
  108.2 0.0 copy-done.4
  108.2 0.3 reshape.53
  108.5 0.5 multiply_reduce_fusion
  109.1 0.0 copy-done.5
  109.1 0.6 multiply_convert_fusion
  109.6 0.7 bitcast_reduce_fusion
  110.4 0.7 fusion.6
  111.0 0.2 copy.18
  111.3 0.8 copy.28
  (2 shorter events, 0.0 us)
Async XLA Ops:
  1.6 1.6 %copy-start = (bf16[512,2048]{1,0:T(8,128)(2,1)S(1)}, bf16[512,2048]{1,0:T(8,128)(2,1)}, u32[]{:S(2)}) copy-start(bf16[512,2048]{1,0:T(8,128)(2,1)} %weight_ref.1) | copy-start | bytes 6291460
  3.2 1.1 %copy-start.1 = (bf16[2,384,512]{2,1,0:T(8,128)(2,1)S(1)}, bf16[2,384,512]{2,1,0:T(8,128)(2,1)}, u32[]{:S(2)}) copy-start(bf16[2,384,512]{2,1,0:T(8,128)(2,1)} %feat_ref.1) | copy-start | bytes 2359300
  4.3 0.7 copy-start.2
  5.0 0.7 copy-start.3
  5.6 102.5 %copy-start.4 = (bf16[448,512]{1,0:T(8,128)(2,1)S(1)}, bf16[448,512]{1,0:T(8,128)(2,1)}, u32[]{:S(2)}) copy-start(bf16[448,512]{1,0:T(8,128)(2,1)} %param.7) | copy-start | bytes 1376260
  5.6 103.4 %copy-start.5 = (f32[128]{0:T(128)S(1)}, f32[128]{0:T(128)}, u32[]{:S(2)}) copy-start(f32[128]{0:T(128)} %param.10) | copy-start | bytes 1540

commit v2 on v1

v2 whole, which is shorter than its diff:
```python
import math

import jax
import jax.numpy as jnp
from jax import lax
from jax.experimental import pallas as pl
from jax.experimental.pallas import tpu as pltpu
from jax.sharding import Mesh
from jax.sharding import PartitionSpec as P

HD = 128
PATCH = 24
PIECES = 12
COPIES = 18
OFFSETS = (0.0, 4.0, 5.5, 7.0, 8.5, 10.0, 11.5, 15.0, 18.0)
QUERY_TIME = 3.9
DP = ("x_lo", "z", "core")
TENSOR = ("y", "x_hi")
MESH = pl.DeviceIdType.MESH


def wrap(value, size):
    return lax.rem(value + 2 * size, size)


def widen(value):
    return value.astype(jnp.float32)


def narrow(value):
    return value.astype(jnp.bfloat16)


def normalize(values_in, gain):
    scale = lax.rsqrt(jnp.mean(values_in * values_in, axis=-1, keepdims=True) + 1e-05)
    return values_in * scale * gain


def body(
    owner_ref, counts_ref, query_hbm, feat_hbm, weight_hbm, q_gain_ref, k_gain_ref, out_hbm,
    query, feat, weight, result, both,
    partner, chosen, first, left0, right0, left1, right1, left, right,
    summed, cross, ready, near, turned, far, spun, side, twin_k, twin_v,
    send_sem, recv_sem, core_send, core_recv, load_sem, store_sem,
):
    x_lo, z, core = lax.axis_index("x_lo"), lax.axis_index("z"), lax.axis_index("core")
    y, x_hi = lax.axis_index("y"), lax.axis_index("x_hi")
    x = x_hi * 4 + x_lo
    samples, tokens = feat_hbm.shape[:2]
    rows = samples * tokens // PIECES
    per_sample = PIECES // samples
    text_len = query_hbm.shape[0] // samples
    heads = query_hbm.shape[1] // HD

    loads = []

    def load(source, target):
        copy = pltpu.make_async_copy(source, target, load_sem.at[len(loads)])
        copy.start()
        loads.append(copy)
        return copy

    feat_loads = [load(feat_hbm.at[j], feat.at[j]) for j in range(samples)]
    weight_load = load(weight_hbm, weight)
    query_load = load(query_hbm, query)

    def at_x(by):
        there = wrap(x + by, 8)
        return {"x_lo": lax.rem(there, 4), "x_hi": there // 4}

    def at_y(by):
        return {"y": wrap(y + by, 8)}

    def at_z(by):
        return {"z": wrap(z + by, 8)}

    other_core = {"core": 1 - core}

    barrier = pltpu.get_barrier_semaphore()
    peers = [at_y(-1), at_y(1), at_x(-2), at_x(2), at_x(-1), at_x(1)]
    peers += [at_z(-1), at_z(1), at_z(-3), at_z(3), other_core]
    for peer in peers:
        pl.semaphore_signal(barrier, inc=1, device_id=peer, device_id_type=MESH)
    pl.semaphore_wait(barrier, len(peers))

    core_copies = []
    for j in range(samples):
        copy = pltpu.make_async_remote_copy(
            src_ref=feat_hbm.at[j], dst_ref=partner.at[j],
            send_sem=core_send.at[j], recv_sem=core_recv.at[j],
            device_id=other_core, device_id_type=MESH,
        )
        copy.start()
        core_copies.append(copy)

    place = z * 2 + core
    plan, valid = [], []
    for j in range(samples):
        shift = owner_ref[j] // samples
        swap = lax.rem(shift, 2)
        low = lax.rem(shift, 16)
        borrow = jnp.where(place < low, 1, 0)
        along_z = lax.rem(lax.rem(shift // 2, 8) + swap * (1 - core), 8)
        along_x = lax.rem(shift // 16 + borrow + 2, 4)
        plan.append((swap, along_z, along_x))
        source = lax.rem(x_lo * 16 + place - shift + 64, 64)
        valid.append(counts_ref[source * samples + j] * PATCH)

    copies = {}

    def send(piece, number, source, target, device):
        copy = pltpu.make_async_remote_copy(
            src_ref=source, dst_ref=target,
            send_sem=send_sem.at[piece * COPIES + number],
            recv_sem=recv_sem.at[piece * COPIES + number],
            device_id=device, device_id_type=MESH,
        )
        copy.start()
        copies[piece, number] = copy

    def arrive(piece, *numbers):
        for number in numbers:
            copies[piece, number].wait_recv()

    def partial(piece, by):
        head = wrap(y + by, 8)
        columns = pl.ds(pl.multiple_of(head * 2 * HD, 2 * HD), 2 * HD)
        return jnp.dot(
            chosen[pl.ds(piece * rows, rows), :], weight[:, columns],
            preferred_element_type=jnp.float32,
        )

    def start_piece(p):
        j = p // per_sample
        if p % per_sample == 0:
            feat_loads[j].wait()
            if j == 0:
                weight_load.wait()
            core_copies[j].wait_recv()
            swapped = jnp.full((tokens, 1), plan[j][0], jnp.int32) == 1
            chosen[pl.ds(j * tokens, tokens), :] = jnp.where(swapped, partner[j], feat[j])
        first[p] = narrow(partial(p, 4))
        send(p, 0, first.at[p, :, pl.ds(0, HD)], left0.at[p], at_y(-1))
        send(p, 1, first.at[p, :, pl.ds(HD, HD)], right0.at[p], at_y(1))

    def second(p):
        to_left, to_right = partial(p, -3), partial(p, 3)
        arrive(p, 0, 1)
        left1[p, :, pl.ds(0, HD)] = narrow(to_left[:, :HD] + widen(left0[p]))
        left1[p, :, pl.ds(HD, HD)] = narrow(to_left[:, HD:])
        send(p, 2, left1.at[p], left.at[p, 0], at_y(-1))
        right1[p, :, pl.ds(0, HD)] = narrow(to_right[:, :HD])
        right1[p, :, pl.ds(HD, HD)] = narrow(to_right[:, HD:] + widen(right0[p]))
        send(p, 3, right1.at[p], right.at[p, 0], at_y(1))

    def later(p, step):
        to_left, to_right = partial(p, step - 3), partial(p, 3 - step)
        arrive(p, 2 * step, 2 * step + 1)
        left[p, step - 1] = narrow(to_left + widen(left[p, step - 1]))
        send(p, 2 * step + 2, left.at[p, step - 1], left.at[p, step], at_y(-1))
        right[p, step - 1] = narrow(to_right + widen(right[p, step - 1]))
        send(p, 2 * step + 3, right.at[p, step - 1], right.at[p, step], at_y(1))

    def own(p):
        mine = partial(p, 0)
        arrive(p, 6, 7)
        summed[p] = narrow(mine + widen(left[p, 2]) + widen(right[p, 2]))
        send(p, 8, summed.at[p], cross.at[p, 0], at_x(2))
        send(p, 9, summed.at[p], cross.at[p, 1], at_x(-2))

    def normed(p):
        arrive(p, 8, 9)
        total = widen(cross[p, 0]) + widen(cross[p, 1])
        ready[p, :, pl.ds(0, HD)] = narrow(normalize(total[:, :HD], k_gain_ref[...]))
        ready[p, :, pl.ds(HD, HD)] = narrow(total[:, HD:])
        send(p, 10, ready.at[p], near.at[p, 0], at_z(1))
        send(p, 11, ready.at[p], near.at[p, 1], at_z(-1))

    def pick(index, options):
        mask = jnp.full((rows, 1), index, jnp.int32)
        chosen_one = options[0]
        for number in range(1, len(options)):
            chosen_one = jnp.where(mask == number, options[number], chosen_one)
        return chosen_one

    def turn_near(p):
        arrive(p, 10, 11)
        s = plan[p // per_sample][1]
        plus = (s == 1) | (s == 4) | (s == 6)
        minus = (s == 2) | (s == 7)
        index = jnp.where(plus, 1, jnp.where(minus, 2, 0))
        turned[p] = pick(index, [ready[p], near[p, 0], near[p, 1]])
        send(p, 12, turned.at[p], far.at[p, 0], at_z(3))
        send(p, 13, turned.at[p], far.at[p, 1], at_z(-3))

    def turn_far(p):
        arrive(p, 12, 13)
        s = plan[p // per_sample][1]
        plus = (s == 2) | (s == 3) | (s == 4)
        minus = (s == 5) | (s == 6)
        index = jnp.where(plus, 1, jnp.where(minus, 2, 0))
        spun[p] = pick(index, [turned[p], far[p, 0], far[p, 1]])
        send(p, 14, spun.at[p], side.at[p, 0], at_x(1))
        send(p, 15, spun.at[p], side.at[p, 1], at_x(-1))
        send(p, 16, spun.at[p, :, pl.ds(0, HD)], twin_k.at[p], at_x(2))
        send(p, 17, spun.at[p, :, pl.ds(HD, HD)], twin_v.at[p], at_x(-2))

    def finish(p):
        arrive(p, 14, 15, 16, 17)
        u = plan[p // per_sample][2]
        for half, twin in enumerate((twin_k, twin_v)):
            part = pl.ds(half * HD, HD)
            both[pl.ds(p * rows, rows), part] = pick(
                u, [spun[p, :, part], side[p, 0, :, part], twin[p], side[p, 1, :, part]]
            )

    def prepare_queries():
        query_load.wait()
        for a in range(heads):
            part = pl.ds(a * HD, HD)
            normed_query = normalize(widen(query[:, part]), q_gain_ref[...])
            query[:, part] = narrow(normed_query / math.sqrt(HD))

    stores = []

    def attend(j):
        held = pl.ds(j * tokens, tokens)
        text = pl.ds(j * text_len, text_len)
        keys, values = both[held, pl.ds(0, HD)], both[held, pl.ds(HD, HD)]
        column = lax.broadcasted_iota(jnp.int32, (text_len, tokens), 1)
        for a in range(heads):
            part = pl.ds(a * HD, HD)
            scores = lax.dot_general(
                query[text, part], keys, (((1,), (1,)), ((), ())),
                preferred_element_type=jnp.float32,
            )
            exponent = jnp.where(column < valid[j], jnp.exp(scores), 0.0)
            weights = narrow(exponent / jnp.sum(exponent, axis=-1, keepdims=True))
            context = jnp.dot(weights, values, preferred_element_type=jnp.float32)
            result[text, part] = narrow(context)
        copy = pltpu.make_async_copy(result.at[text], out_hbm.at[text], store_sem.at[j])
        copy.start()
        stores.append(copy)

    stages = [start_piece, second, lambda p: later(p, 1), lambda p: later(p, 2), own, normed]
    stages += [turn_near, turn_far, finish]
    tasks = [(QUERY_TIME, 1, prepare_queries, ())]
    for number, (stage, offset) in enumerate(zip(stages, OFFSETS)):
        tasks += [(p + offset, -number, stage, (p,)) for p in range(PIECES)]
    for j in range(samples):
        tasks.append(((j + 1) * per_sample - 1 + OFFSETS[-1], 1, attend, (j,)))
    for _, _, task, given in sorted(tasks, key=lambda task: task[:2]):
        task(*given)
    for copy in core_copies + list(copies.values()):
        copy.wait_send()
    for copy in stores:
        copy.wait()


def shards(queries, features, kv_weight, q_gain, k_gain, counts, owner):
    samples, tokens, width = features.shape
    total = samples * tokens
    rows = total // PIECES
    wide, half = (rows, 2 * HD), (rows, HD)

    def whole(*shape):
        return pltpu.VMEM(shape, jnp.bfloat16)

    def buffers(*shape):
        return whole(PIECES, *shape)

    smem = pl.BlockSpec(memory_space=pltpu.SMEM)
    vmem = pl.BlockSpec(memory_space=pltpu.VMEM)
    hbm = pl.BlockSpec(memory_space=pltpu.HBM)
    return pl.pallas_call(
        body,
        out_shape=jax.ShapeDtypeStruct(queries.shape, jnp.bfloat16),
        in_specs=[smem, smem, hbm, hbm, hbm, vmem, vmem],
        out_specs=hbm,
        scratch_shapes=[
            whole(*queries.shape), whole(*features.shape), whole(*kv_weight.shape),
            whole(*queries.shape), whole(total, 2 * HD),
            whole(samples, tokens, width), whole(total, width),
            buffers(*wide), buffers(*half), buffers(*half), buffers(*wide), buffers(*wide),
            buffers(3, *wide), buffers(3, *wide),
            buffers(*wide), buffers(2, *wide), buffers(*wide), buffers(2, *wide),
            buffers(*wide), buffers(2, *wide), buffers(*wide), buffers(2, *wide),
            buffers(*half), buffers(*half),
            pltpu.SemaphoreType.DMA((PIECES * COPIES,)),
            pltpu.SemaphoreType.DMA((PIECES * COPIES,)),
            pltpu.SemaphoreType.DMA((samples,)),
            pltpu.SemaphoreType.DMA((samples,)),
            pltpu.SemaphoreType.DMA((samples + 2,)),
            pltpu.SemaphoreType.DMA((samples,)),
        ],
        compiler_params=pltpu.CompilerParams(
            collective_id=0, has_side_effects=True, vmem_limit_bytes=60 * 1024 * 1024
        ),
        name="exchange",
    )(
        owner, counts, queries, features, kv_weight, q_gain.reshape(1, HD), k_gain.reshape(1, HD)
    )


def solution(mesh):
    torus = Mesh(mesh.devices.reshape(4, 8, 2, 8, 2), (*DP, *TENSOR))
    in_specs = (P(DP, TENSOR), P(DP, None, TENSOR), P(TENSOR, None), P(), P(), P(), P())
    return jax.shard_map(
        shards, mesh=torus, in_specs=in_specs, out_specs=P(DP, TENSOR), check_vma=False
    )
```

time: 112 us -> 96 us (0.86); the launches traced: 112 us -> 94.6 us
  Pallas kernels: 103 us -> 92.8 us
  local copies, waits for them, and re-layouts: 5.4 us -> 1.82 us
  other arithmetic: 2.73 us -> 0 us
  matrix products: 1.38 us -> 0 us
    pallas_call x1, Pallas kernels: 103 us -> 92.8 us  [shards(): pl.pallas_call(body, out_shape=jax.ShapeDtypeStruct(queries.shape, jnp.bf...]
    unnamed x13 -> x1, local copies, waits for them, and re-layouts: 4.88 us -> 1.82 us
    dot_general x2 -> x0, matrix products: 1.38 us -> none  [the longest x1 0.71 us: shards(): jnp.einsum('stad,srd->satr', query_normed, key_heads, preferred_element_t...]
    reduce_sum x2 -> x0, other arithmetic: 1.38 us -> none  [the longest x1 0.84 us: shards(): slot_count = jnp.sum(jnp.where(matches, counts[None, :], 0), axis=1)]
where the time goes in v2:
time: 96 us; the launch traced here: 94.6 us
  Pallas kernels  92.8 us (97%)
  local copies, waits for them, and re-layouts  1.82 us (2%)
    pallas_call x1, Pallas kernels, shards(): pl.pallas_call(body, out_shape=jax.ShapeDtypeStruct(queries.shape, jnp.bf...  92.8 us

profile of v2, /device:TPU:14, one launch (start us, length us, event | category | flops | bytes accessed | tf_op | source)
XLA Modules:
  0.0 94.6 jit_solution(7063468757744368667)
XLA Ops:
  0.0 92.8 %exchange.1 = bf16[448,512]{1,0:T(8,128)(2,1)} custom-call(s32[128]{0:T(128)} %owner_ref.1, s32[128]{0:T(128)} %counts_ref.1, bf16[448,512]{1,0:T(8,128)(2,1)} %query_hbm.1, bf16[2,384,512]{2,1,0:T(8,128)(2,1)} %feat_hbm.1, bf16[512,2048]{1,0:T(8,128)(2,1)} %weight_hbm.1, f32[1,128]{1,0:T(1,128)} %bitcast.2, f32[1,128]{1,0:T(1,128)} %bitcast.3), custom_call_target="tpu_custom_call" | custom-call | tf_op jit(solution)/shard_map/exchange/pallas_call | solution.py:275
  92.8 1.8 %copy.9 = bf16[448,512]{1,0:T(8,128)(2,1)} copy(bf16[448,512]{1,0:T(8,128)(2,1)} %exchange.1) | data formatting | bytes 917504

commit v3 on v2

--- a/solution.py
+++ b/solution.py
@@ -10,10 +10,10 @@
 
 HD = 128
 PATCH = 24
-PIECES = 12
+PIECES = 8
 COPIES = 18
-OFFSETS = (0.0, 4.0, 5.5, 7.0, 8.5, 10.0, 11.5, 15.0, 18.0)
-QUERY_TIME = 3.9
+OFFSETS = (0.0, 7.0, 8.0, 9.0, 9.5, 11.0, 12.5, 14.5, 16.5)
+QUERY_TIME = 6.9
 DP = ("x_lo", "z", "core")
 TENSOR = ("y", "x_hi")
 MESH = pl.DeviceIdType.MESH

time: 96 us -> 99.9 us (1.041)
  Pallas kernels: 92.8 us -> 96.7 us
    pallas_call x1, Pallas kernels: 92.8 us -> 96.7 us  [shards(): pl.pallas_call(body, out_shape=jax.ShapeDtypeStruct(queries.shape, jnp.bf...]
where the time goes in v3:
time: 99.9 us; the launch traced here: 98.6 us
  Pallas kernels  96.7 us (97%)
  local copies, waits for them, and re-layouts  1.82 us (2%)
    pallas_call x1, Pallas kernels, shards(): pl.pallas_call(body, out_shape=jax.ShapeDtypeStruct(queries.shape, jnp.bf...  96.7 us

profile of v3, /device:TPU:14, one launch (start us, length us, event | category | flops | bytes accessed | tf_op | source)
XLA Modules:
  0.0 98.6 jit_solution(1011294178579037192)
XLA Ops:
  0.0 96.7 %exchange.1 = bf16[448,512]{1,0:T(8,128)(2,1)} custom-call(s32[128]{0:T(128)} %owner_ref.1, s32[128]{0:T(128)} %counts_ref.1, bf16[448,512]{1,0:T(8,128)(2,1)} %query_hbm.1, bf16[2,384,512]{2,1,0:T(8,128)(2,1)} %feat_hbm.1, bf16[512,2048]{1,0:T(8,128)(2,1)} %weight_hbm.1, f32[1,128]{1,0:T(1,128)} %bitcast.2, f32[1,128]{1,0:T(1,128)} %bitcast.3), custom_call_target="tpu_custom_call" | custom-call | tf_op jit(solution)/shard_map/exchange/pallas_call | solution.py:275
  96.7 1.8 %copy.9 = bf16[448,512]{1,0:T(8,128)(2,1)} copy(bf16[448,512]{1,0:T(8,128)(2,1)} %exchange.1) | data formatting | bytes 917504
